TPU v7x, 16 devices: a whole 2x2x2 slice. The times are simulated.
16 devices in a mesh: dp: 2 (over z), ep: 8 (over y, x, core).
Axes of the slice: x: 2, y: 2, z: 2, core: 2. Of those that a mesh axis runs over, the one named last changes fastest.
Arguments:
- tok_x: bfloat16 [16384, 4096], P(('dp', 'ep'))
- tok_dy: bfloat16 [16384, 4096], P(('dp', 'ep'))
- exp_first: int32 [16384], P(('dp', 'ep'))
- exp_second: int32 [16384], P(('dp', 'ep'))
- eligible: int32 [16384, 8], P(('dp', 'ep'))
- slot_first: int32 [16384], P(('dp', 'ep'))
- slot_second: int32 [16384], P(('dp', 'ep'))
- ln_weight: bfloat16 [4096], replicated
- ln_bias: bfloat16 [4096], replicated
- router: bfloat16 [4096, 8], replicated
- w_gate: bfloat16 [8, 4096, 1376], P('ep')
- w_up: bfloat16 [8, 4096, 1376], P('ep')
- w_down: bfloat16 [8, 1376, 4096], P('ep')
Outputs:
- output 1: bfloat16 [16384, 4096], P(('dp', 'ep'))
- output 2: bfloat16 [16384, 4096], P(('dp', 'ep'))
- output 3: float32 [8, 4096, 1376], P('ep')
- output 4: float32 [8, 4096, 1376], P('ep')
- output 5: float32 [8, 1376, 4096], P('ep')
- output 6: float32 [4096, 8], replicated
- output 7: float32 [4096], replicated
- output 8: float32 [4096], replicated
All inputs are finite; a program needn't handle non-finite values.
Results may differ from a plain program's by a relative error of at most 0.00493557.
Values are sent between devices in bfloat16 or wider.
A program may use at most 1 GiB of HBM per device.

v0:
```python
import jax
import jax.numpy as jnp
from jax import lax
from jax.sharding import PartitionSpec as P

LN_EPS = 1e-5


def layer_norm(x_rows, ln_weight, ln_bias):
    x_float = x_rows.astype(jnp.float32)
    centered = x_float - jnp.mean(x_float, axis=-1, keepdims=True)
    inv_std = lax.rsqrt(jnp.mean(centered * centered, axis=-1, keepdims=True) + LN_EPS)
    x_hat = centered * inv_std
    hidden = (x_hat * ln_weight.astype(jnp.float32) + ln_bias.astype(jnp.float32)).astype(jnp.bfloat16)
    return hidden, x_hat, inv_std


def layer_norm_back(grad_h, x_hat, inv_std, ln_weight):
    scaled = grad_h * ln_weight.astype(jnp.float32)
    return inv_std * (scaled - jnp.mean(scaled, axis=-1, keepdims=True)
                      - x_hat * jnp.mean(scaled * x_hat, axis=-1, keepdims=True))


def masked_gate(logits, allowed, choice):
    expert_ids = jnp.arange(logits.shape[-1])
    prob_all = jax.nn.softmax(jnp.where(allowed, logits, -1e30), axis=-1)
    picked = (choice[:, None] == expert_ids[None, :]).astype(jnp.float32)
    return jnp.sum(prob_all * picked, axis=-1), prob_all, picked


def solution(mesh):
    n_ep = mesh.shape['ep']
    tok_spec = P(('dp', 'ep'), None)
    row_spec = P(('dp', 'ep'))
    exp_spec = P('ep', None, None)

    def local_step(tok_x, tok_dy, exp_first, exp_second, eligible, slot_first, slot_second,
                   ln_weight, ln_bias, router, w_gate, w_up, w_down):
        n_local, d_model = tok_x.shape
        n_exp = eligible.shape[1]
        local_exp = w_gate.shape[0]
        slot_cap = 3 * n_local // n_exp
        f32 = jnp.float32
        hidden, x_hat, inv_std = layer_norm(tok_x, ln_weight, ln_bias)
        logits = jnp.dot(hidden, router, preferred_element_type=f32)
        expert_ids = jnp.arange(n_exp)
        allowed = eligible > 0
        gate_one, prob_one, pick_one = masked_gate(logits, allowed, exp_first)
        gate_two, prob_two, pick_two = masked_gate(logits, allowed & (expert_ids[None, :] != exp_first[:, None]), exp_second)
        row_ids = jnp.arange(n_exp * slot_cap)
        pos_one = jnp.where(slot_first >= 0, exp_first * slot_cap + slot_first, -1)
        pos_two = jnp.where(slot_second >= 0, exp_second * slot_cap + slot_second, -1)
        sel_one = (pos_one[:, None] == row_ids[None, :]).astype(jnp.bfloat16)
        sel_two = (pos_two[:, None] == row_ids[None, :]).astype(jnp.bfloat16)
        sel_both = sel_one + sel_two
        hid_buf = jnp.einsum('tp,td->pd', sel_both, hidden, preferred_element_type=f32).astype(jnp.bfloat16)
        hid_recv = lax.all_to_all(hid_buf.reshape(n_ep, local_exp, slot_cap, d_model), 'ep', 0, 0, tiled=True)
        pre_gate = jnp.einsum('sgcd,gdf->sgcf', hid_recv, w_gate, preferred_element_type=f32)
        pre_up = jnp.einsum('sgcd,gdf->sgcf', hid_recv, w_up, preferred_element_type=f32)
        sig_gate = jax.nn.sigmoid(pre_gate)
        silu_gate = pre_gate * sig_gate
        inner_act = (silu_gate * pre_up).astype(jnp.bfloat16)
        exp_out = jnp.einsum('sgcf,gfd->sgcd', inner_act, w_down, preferred_element_type=f32).astype(jnp.bfloat16)
        out_back = lax.all_to_all(exp_out, 'ep', 0, 0, tiled=True).reshape(n_exp * slot_cap, d_model)
        out_one = jnp.dot(sel_one, out_back, preferred_element_type=f32)
        out_two = jnp.dot(sel_two, out_back, preferred_element_type=f32)
        y_mix = gate_one[:, None] * out_one + gate_two[:, None] * out_two
        out_tok = (tok_x.astype(f32) + y_mix).astype(jnp.bfloat16)
        dy_float = tok_dy.astype(f32)
        grad_one = (gate_one[:, None] * dy_float).astype(jnp.bfloat16)
        grad_two = (gate_two[:, None] * dy_float).astype(jnp.bfloat16)
        grad_buf = (jnp.einsum('tp,td->pd', sel_one, grad_one, preferred_element_type=f32)
                    + jnp.einsum('tp,td->pd', sel_two, grad_two, preferred_element_type=f32)).astype(jnp.bfloat16)
        grad_recv = lax.all_to_all(grad_buf.reshape(n_ep, local_exp, slot_cap, d_model), 'ep', 0, 0, tiled=True)
        grad_inner = jnp.einsum('sgcd,gfd->sgcf', grad_recv, w_down, preferred_element_type=f32)
        dw_down = jnp.einsum('sgcf,sgcd->gfd', inner_act, grad_recv, preferred_element_type=f32)
        grad_pre_gate = (grad_inner * pre_up * sig_gate * (1.0 + pre_gate * (1.0 - sig_gate))).astype(jnp.bfloat16)
        grad_pre_up = (grad_inner * silu_gate).astype(jnp.bfloat16)
        dw_gate = jnp.einsum('sgcd,sgcf->gdf', hid_recv, grad_pre_gate, preferred_element_type=f32)
        dw_up = jnp.einsum('sgcd,sgcf->gdf', hid_recv, grad_pre_up, preferred_element_type=f32)
        grad_hid = (jnp.einsum('sgcf,gdf->sgcd', grad_pre_gate, w_gate, preferred_element_type=f32)
                    + jnp.einsum('sgcf,gdf->sgcd', grad_pre_up, w_up, preferred_element_type=f32)).astype(jnp.bfloat16)
        hid_back = lax.all_to_all(grad_hid, 'ep', 0, 0, tiled=True).reshape(n_exp * slot_cap, d_model)
        grad_exp = jnp.dot(sel_both, hid_back, preferred_element_type=f32)
        dgate_one = jnp.sum(dy_float * out_one, axis=-1)
        dgate_two = jnp.sum(dy_float * out_two, axis=-1)
        d_logits = ((dgate_one * gate_one)[:, None] * (pick_one - prob_one)
                    + (dgate_two * gate_two)[:, None] * (pick_two - prob_two)).astype(jnp.bfloat16)
        d_router = jnp.einsum('td,te->de', hidden, d_logits, preferred_element_type=f32)
        grad_h = jnp.einsum('te,de->td', d_logits, router, preferred_element_type=f32) + grad_exp
        d_ln_weight = jnp.sum(grad_h * x_hat, axis=0)
        d_ln_bias = jnp.sum(grad_h, axis=0)
        dx_tok = (dy_float + layer_norm_back(grad_h, x_hat, inv_std, ln_weight)).astype(jnp.bfloat16)
        dw_gate = lax.psum(dw_gate, 'dp')
        dw_up = lax.psum(dw_up, 'dp')
        dw_down = lax.psum(dw_down, 'dp')
        d_router = lax.psum(d_router, ('dp', 'ep'))
        d_ln_weight = lax.psum(d_ln_weight, ('dp', 'ep'))
        d_ln_bias = lax.psum(d_ln_bias, ('dp', 'ep'))
        return out_tok, dx_tok, dw_gate, dw_up, dw_down, d_router, d_ln_weight, d_ln_bias

    return jax.shard_map(
        local_step, mesh=mesh,
        in_specs=(tok_spec, tok_spec, row_spec, row_spec, tok_spec, row_spec, row_spec,
                  P(), P(), P(), exp_spec, exp_spec, exp_spec),
        out_specs=(tok_spec, tok_spec, exp_spec, exp_spec, exp_spec, P(), P(), P()),
        check_vma=False)
```

profile of v0, /device:TPU:0, one launch (start us, length us, event | category | flops | bytes accessed | tf_op | source)
XLA Modules:
  0.0 2759.4 jit_solution(8355858997787501027)
XLA Ops:
  29.1 32.4 %fusion.52 = f32[3072,4096]{1,0:T(8,128)} fusion(bf16[1024,4096]{1,0:T(8,128)(2,1)S(1)} %bitcast.160, f32[1024]{0:T(1024)S(1)} %get-tuple-element.14, s32[1024]{0:T(1024)S(1)} %get-tuple-element.32), kind=kOutput, calls=%fused_computation.67 | convolution fusion | flops 25785532416 | bytes 58728448 | tf_op jit(solution)/shard_map/tp,td->pd/dot_general | solution.py:72
  61.5 38.4 %add_convert_fusion.1 = bf16[3072,4096]{1,0:T(8,128)(2,1)} fusion(f32[3072,4096]{1,0:T(8,128)} %fusion.52, bf16[1024,4096]{1,0:T(8,128)(2,1)} %param.14, f32[1024]{0:T(1024)S(1)} %select_reduce_fusion, s32[1024]{0:T(1024)S(1)} %get-tuple-element.31), kind=kOutput, calls=%fused_computation.1 | convolution fusion | flops 25810698240 | bytes 83894272 | tf_op jit(solution)/shard_map/tp,td->pd/dot_general | solution.py:73
  106.3 34.3 %convolution_convert_fusion = bf16[3072,4096]{1,0:T(8,128)(2,1)} fusion(bf16[1024,4096]{1,0:T(8,128)(2,1)} %copy-done.1, s32[1024]{0:T(1024)S(1)} %get-tuple-element.31, s32[1024]{0:T(1024)S(1)} %get-tuple-element.32), kind=kOutput, calls=%fused_computation.24 | convolution fusion | flops 25807552512 | bytes 33562624 | tf_op jit(solution)/shard_map/tp,td->pd/dot_general | solution.py:56
  140.6 240.6 %all-to-all-done.2 = bf16[8,1,384,4096]{3,2,1,0:T(8,128)(2,1)} async-done(((bf16[8,1,384,4096]{3,2,1,0:T(8,128)(2,1)}), bf16[8,1,384,4096]{3,2,1,0:T(8,128)(2,1)}, u32[]{:S(2)}, u32[]{:S(2)}) %all-to-all-start.2) | async-done | bytes 25165856 | tf_op jit(solution)/shard_map/all_to_all | solution.py:74
  387.8 44.1 %fusion.3 = f32[8,384,1376]{1,2,0:T(8,128)} fusion(bf16[8,1,384,4096]{3,2,1,0:T(8,128)(2,1)} %all-to-all-done.2, bf16[1,1376,4096]{2,1,0:T(8,128)(2,1)} %param.25), kind=kOutput, calls=%fused_computation.10 | convolution fusion | flops 34628173824 | bytes 53346304 | tf_op jit(solution)/shard_map/sgcd,gfd->sgcf/dot_general | solution.py:75
  431.9 229.9 %all-to-all-done = bf16[8,1,384,4096]{3,2,1,0:T(8,128)(2,1)} async-done(((bf16[8,1,384,4096]{3,2,1,0:T(8,128)(2,1)}), bf16[8,1,384,4096]{3,2,1,0:T(8,128)(2,1)}, u32[]{:S(2)}, u32[]{:S(2)}) %all-to-all-start) | async-done | bytes 25165856 | tf_op jit(solution)/shard_map/all_to_all | solution.py:57
  661.8 44.3 %fusion.9 = f32[8,384,1376]{1,2,0:T(8,128)} fusion(bf16[8,1,384,4096]{3,2,1,0:T(8,128)(2,1)} %all-to-all-done, bf16[1,4096,1376]{1,2,0:T(8,128)(2,1)} %param.24), kind=kOutput, calls=%fused_computation.16 | convolution fusion | flops 34628173824 | bytes 53346304 | tf_op jit(solution)/shard_map/sgcd,gdf->sgcf/dot_general | solution.py:59
  706.0 64.7 %fusion.63 = (bf16[8,384,1376]{1,2,0:T(8,128)(2,1)}, bf16[8,1,384,1376]{2,3,0,1:T(8,128)(2,1)}, bf16[8,384,1376]{1,2,0:T(8,128)(2,1)}) fusion(f32[8,384,1376]{1,2,0:T(8,128)} %fusion.3, f32[8,384,1376]{1,2,0:T(8,128)} %fusion.9, bf16[1,4096,1376]{1,2,0:T(8,128)(2,1)} %param.23, bf16[8,1,384,4096]{3,2,1,0:T(8,128)(2,1)} %all-to-all-done), kind=kOutput, calls=%fused_computation.79 | convolution fusion | flops 34691579904 | bytes 95617024 | tf_op jit(solution)/shard_map/sgcd,gdf->sgcf/dot_general | solution.py:58
  770.8 46.1 %convert_bitcast_fusion = bf16[8,1,384,4096]{3,2,1,0:T(8,128)(2,1)} fusion(bf16[8,384,1376]{1,2,0:T(8,128)(2,1)} %get-tuple-element.27, bf16[1,1376,4096]{2,1,0:T(8,128)(2,1)S(1)} %copy-done.52), kind=kOutput, calls=%fused_computation.20 | convolution fusion | flops 34640756736 | bytes 44892160 | tf_op jit(solution)/shard_map/sgcf,gfd->sgcd/dot_general | solution.py:63
  823.4 43.7 %fusion.25 = f32[1,1376,4096]{2,1,0:T(8,128)} fusion(bf16[8,384,1376]{1,2,0:T(8,128)(2,1)} %get-tuple-element.27, bf16[8,1,384,4096]{3,2,1,0:T(8,128)(2,1)} %all-to-all-done.2), kind=kOutput, calls=%fused_computation.33 | convolution fusion | flops 34628173824 | bytes 56164352 | tf_op jit(solution)/shard_map/sgcf,sgcd->gfd/dot_general | solution.py:76
  867.1 43.7 %fusion.19 = f32[1,4096,1376]{1,2,0:T(8,128)} fusion(bf16[8,384,1376]{1,2,0:T(8,128)(2,1)} %get-tuple-element.25, bf16[8,1,384,4096]{3,2,1,0:T(8,128)(2,1)} %all-to-all-done), kind=kOutput, calls=%fused_computation.31 | convolution fusion | flops 34628173824 | bytes 56164352 | tf_op jit(solution)/shard_map/sgcd,sgcf->gdf/dot_general | solution.py:80
  910.8 186.5 %all-to-all-done.1 = bf16[8,1,384,4096]{3,2,1,0:T(8,128)(2,1)} async-done(((bf16[8,1,384,4096]{3,2,1,0:T(8,128)(2,1)}), bf16[8,1,384,4096]{3,2,1,0:T(8,128)(2,1)}, u32[]{:S(2)}, u32[]{:S(2)}) %all-to-all-start.1) | async-done | bytes 25165856 | tf_op jit(solution)/shard_map/all_to_all | solution.py:64
  1097.3 31.9 %fusion.50 = f32[1024,4096]{1,0:T(8,128)} fusion(bf16[3072,4096]{1,0:T(8,128)(2,1)} %bitcast.22, s32[1024]{0:T(1024)S(1)} %copy-done.47), kind=kOutput, calls=%fused_computation.64 | convolution fusion | flops 25772949504 | bytes 41947136 | tf_op jit(solution)/shard_map/dot_general | solution.py:66
  1129.3 36.8 %fusion.45 = (f32[1024]{0:T(1024)S(1)}, f32[1024]{0:T(1024)S(1)}, bf16[1024,4096]{1,0:T(8,128)(2,1)}) fusion(bf16[1024,4096]{1,0:T(8,128)(2,1)} %param.14, f32[1024,4096]{1,0:T(8,128)} %fusion.50, f32[1024]{0:T(1024)S(1)} %copy-done.41, f32[1024]{0:T(1024)S(1)} %copy-done.39, bf16[1024,4096]{1,0:T(8,128)(2,1)} %param.13, bf16[3072,4096]{1,0:T(8,128)(2,1)} %bitcast.22, ...), kind=kOutput, calls=%fused_computation.57 | convolution fusion | flops 25819086848 | bytes 67129344 | tf_op jit(solution)/shard_map/dot_general | solution.py:65
  1172.6 43.7 %fusion.22 = f32[1,4096,1376]{1,2,0:T(8,128)} fusion(bf16[8,1,384,4096]{3,2,1,0:T(8,128)(2,1)} %all-to-all-done, bf16[8,1,384,1376]{2,3,0,1:T(8,128)(2,1)} %get-tuple-element.26), kind=kOutput, calls=%fused_computation.32 | convolution fusion | flops 34628173824 | bytes 56164352 | tf_op jit(solution)/shard_map/sgcd,sgcf->gdf/dot_general | solution.py:79
  1216.3 48.8 %fusion.59 = f32[8,384,4096]{2,1,0:T(8,128)} fusion(bf16[1,4096,1376]{1,2,0:T(8,128)(2,1)} %param.23, bf16[8,1,384,1376]{2,3,0,1:T(8,128)(2,1)} %get-tuple-element.26), kind=kOutput, calls=%fused_computation.74 | convolution fusion | flops 34628173824 | bytes 70057984 | tf_op jit(solution)/shard_map/sgcf,gdf->sgcd/dot_general | solution.py:81
  1265.1 50.1 %fusion = bf16[8,1,384,4096]{3,2,1,0:T(8,128)(2,1)} fusion(f32[8,384,4096]{2,1,0:T(8,128)} %fusion.59, bf16[8,384,1376]{1,2,0:T(8,128)(2,1)} %get-tuple-element.25, bf16[1,4096,1376]{1,2,0:T(8,128)(2,1)} %param.24), kind=kOutput, calls=%fused_computation.7 | convolution fusion | flops 34653339648 | bytes 95223808 | tf_op jit(solution)/shard_map/sgcf,gdf->sgcd/dot_general | solution.py:82
  1315.2 283.4 %all_to_all.20 = bf16[8,1,384,4096]{3,2,1,0:T(8,128)(2,1)} all-to-all(bf16[8,1,384,4096]{3,2,1,0:T(8,128)(2,1)} %fusion), channel_id=1, replica_groups=mesh['dp'=2,'ep'=8] {'ep'}, dimensions={0} | all-to-all | bytes 50331648 | tf_op jit(solution)/shard_map/all_to_all | solution.py:83
  1598.7 32.0 %fusion.71 = f32[1024,4096]{1,0:T(8,128)} fusion(bf16[3072,4096]{1,0:T(8,128)(2,1)} %bitcast.156, s32[1024]{0:T(1024)S(1)} %copy-done.48, s32[1024]{0:T(1024)S(1)} %copy-done.51), kind=kOutput, calls=%fused_computation.85 | convolution fusion | flops 25794969600 | bytes 41951232 | tf_op jit(solution)/shard_map/dot_general | solution.py:84
  1645.8 34.1 %all-reduce = (f32[4096]{0:T(1024)}, f32[4096]{0:T(1024)}) all-reduce(f32[4096]{0:T(1024)S(1)} %get-tuple-element.8, f32[4096]{0:T(1024)S(1)} %get-tuple-element.11), channel_id=1, replica_groups=mesh['dp'=2,'ep'=8] {'dp','ep'}, use_global_device_ids=true, to_apply=%region_17.18 | all-reduce | flops 8192 | bytes 65536 | tf_op jit(solution)/shard_map/psum | solution.py:98
  1680.0 16.4 fusion.49
  1696.4 1010.6 %all-reduce.7.cloned.1.call-done = (f32[1,4096,1376]{1,2,0:T(8,128)}, f32[1,4096,1376]{1,2,0:T(8,128)}, f32[1,1376,4096]{2,1,0:T(8,128)}) async-done(((f32[1,4096,1376]{1,2,0:T(8,128)}, f32[1,4096,1376]{1,2,0:T(8,128)}, f32[1,1376,4096]{2,1,0:T(8,128)}), (f32[1,4096,1376]{1,2,0:T(8,128)}, f32[1,4096,1376]{1,2,0:T(8,128)}, f32[1,1376,4096]{2,1,0:T(8,128)})) %all-reduce.7.cloned.1.call-update) | async-done | bytes 67633168 | tf_op jit(solution)/shard_map/psum | solution.py:94
  2707.0 18.1 copy.29
  2725.1 18.1 copy.30
  (162 shorter events, 71.3 us)
Async XLA Ops:
  28.4 33.1 %copy-start.38 = (f32[1024]{0:T(1024)}, f32[1024]{0:T(1024)S(1)}, u32[]{:S(2)}) copy-start(f32[1024]{0:T(1024)S(1)} %get-tuple-element.14) | copy-start | bytes 12292
  29.0 77.3 %copy-start.46 = (s32[1024]{0:T(1024)}, s32[1024]{0:T(1024)S(1)}, u32[]{:S(2)}) copy-start(s32[1024]{0:T(1024)S(1)} %get-tuple-element.31) | copy-start | bytes 12292
  29.0 77.3 %copy-start.49 = (s32[1024]{0:T(1024)}, s32[1024]{0:T(1024)S(1)}, u32[]{:S(2)}) copy-start(s32[1024]{0:T(1024)S(1)} %get-tuple-element.32) | copy-start | bytes 12292
  99.9 281.3 %all-to-all-start.2 = ((bf16[8,1,384,4096]{3,2,1,0:T(8,128)(2,1)}), bf16[8,1,384,4096]{3,2,1,0:T(8,128)(2,1)}, u32[]{:S(2)}, u32[]{:S(2)}) async-start(bf16[8,1,384,4096]{3,2,1,0:T(8,128)(2,1)} %bitcast.155), calls=%async_computation.2 | async-start | bytes 50331648 | tf_op jit(solution)/shard_map/all_to_all | solution.py:74
  381.2 280.6 %all-to-all-start = ((bf16[8,1,384,4096]{3,2,1,0:T(8,128)(2,1)}), bf16[8,1,384,4096]{3,2,1,0:T(8,128)(2,1)}, u32[]{:S(2)}, u32[]{:S(2)}) async-start(bf16[8,1,384,4096]{3,2,1,0:T(8,128)(2,1)} %bitcast.154), calls=%async_computation | async-start | bytes 50331648 | tf_op jit(solution)/shard_map/all_to_all | solution.py:57
  706.0 64.7 %copy-start.52 = (bf16[1,1376,4096]{2,1,0:T(8,128)(2,1)S(1)}, bf16[1,1376,4096]{2,1,0:T(8,128)(2,1)}, u32[]{:S(2)}) copy-start(bf16[1,1376,4096]{2,1,0:T(8,128)(2,1)} %param.25) | copy-start | bytes 33816580
  816.9 280.4 %all-to-all-start.1 = ((bf16[8,1,384,4096]{3,2,1,0:T(8,128)(2,1)}), bf16[8,1,384,4096]{3,2,1,0:T(8,128)(2,1)}, u32[]{:S(2)}, u32[]{:S(2)}) async-start(bf16[8,1,384,4096]{3,2,1,0:T(8,128)(2,1)} %convert_bitcast_fusion), calls=%async_computation.1 | async-start | bytes 50331648 | tf_op jit(solution)/shard_map/all_to_all | solution.py:64
  823.3 873.1 %all-reduce.5.cloned.1.call-start = ((), (), s32[]{:S(2)}) async-start(), calls=%async_computation.4 | async-start | bytes 262144 | tf_op jit(solution)/shard_map/psum | solution.py:97
  867.1 230.2 %copy-start.47 = (s32[1024]{0:T(1024)S(1)}, s32[1024]{0:T(1024)}, u32[]{:S(2)}) copy-start(s32[1024]{0:T(1024)} %copy-done.46) | copy-start | bytes 12292
  1129.2 38.0 %copy-start.3 = (f32[1024,8]{0,1:T(8,128)S(1)}, f32[1024,8]{0,1:T(8,128)}, u32[]{:S(2)}) copy-start(f32[1024,8]{0,1:T(8,128)} %copy-done.2) | copy-start | bytes 98308
  1129.2 38.0 %copy-start.6 = (pred[1024,8]{0,1:T(8,128)(4,1)S(1)}, pred[1024,8]{0,1:T(8,128)(4,1)}, u32[]{:S(2)}) copy-start(pred[1024,8]{0,1:T(8,128)(4,1)} %copy-done.5) | copy-start | bytes 24580
  1129.2 38.0 %copy-start.12 = (s32[1024]{0:T(1024)S(1)}, s32[1024]{0:T(1024)}, u32[]{:S(2)}) copy-start(s32[1024]{0:T(1024)} %param.15) | copy-start | bytes 12292
  1129.2 38.0 %copy-start.15 = (f32[1024]{0:T(1024)S(1)}, f32[1024]{0:T(1024)}, u32[]{:S(2)}) copy-start(f32[1024]{0:T(1024)} %copy-done.14) | copy-start | bytes 12292
  1129.2 38.0 %copy-start.18 = (f32[1024]{0:T(1024)S(1)}, f32[1024]{0:T(1024)}, u32[]{:S(2)}) copy-start(f32[1024]{0:T(1024)} %copy-done.17) | copy-start | bytes 12292
  1129.2 38.0 %copy-start.24 = (f32[1024]{0:T(1024)S(1)}, f32[1024]{0:T(1024)}, u32[]{:S(2)}) copy-start(f32[1024]{0:T(1024)} %copy-done.23) | copy-start | bytes 12292
  1129.3 38.0 %copy-start.27 = (f32[1024]{0:T(1024)S(1)}, f32[1024]{0:T(1024)}, u32[]{:S(2)}) copy-start(f32[1024]{0:T(1024)} %copy-done.26) | copy-start | bytes 12292
  1129.3 38.0 %copy-start.30 = (s32[1024]{0:T(1024)S(1)}, s32[1024]{0:T(1024)}, u32[]{:S(2)}) copy-start(s32[1024]{0:T(1024)} %param.16) | copy-start | bytes 12292
  1172.5 1534.4 %all-reduce.7.cloned.1.call-start = ((), (), s32[]{:S(2)}) async-start(), calls=%async_computation.5 | async-start | bytes 135266304 | tf_op jit(solution)/shard_map/psum | solution.py:94
  1315.2 283.4 %copy-start.48 = (s32[1024]{0:T(1024)S(1)}, s32[1024]{0:T(1024)}, u32[]{:S(2)}) copy-start(s32[1024]{0:T(1024)} %copy-done.46) | copy-start | bytes 12292
  1315.2 283.4 %copy-start.51 = (s32[1024]{0:T(1024)S(1)}, s32[1024]{0:T(1024)}, u32[]{:S(2)}) copy-start(s32[1024]{0:T(1024)} %copy-done.49) | copy-start | bytes 12292
  1315.2 315.6 %slice-start.2 = ((s8[8388608]{0:T(1024)(128)(4,1)}), s8[4194304]{0:T(1024)(128)(4,1)S(1)}, s32[]{:S(2)}) async-start(s8[8388608]{0:T(1024)(128)(4,1)} %bitcast.152), calls=%async_computation.8 | async-start | bytes 8388608
  2707.0 36.3 %slice-start.4 = ((s8[22544384]{0:T(1024)(128)(4,1)}), s8[4194304]{0:T(1024)(128)(4,1)S(1)}, s32[]{:S(2)}) async-start(s8[22544384]{0:T(1024)(128)(4,1)} %bitcast.157), calls=%async_computation.10 | async-start | bytes 8388608
  2707.0 36.3 %slice-start.5 = ((s8[22544384]{0:T(1024)(128)(4,1)}), s8[4194304]{0:T(1024)(128)(4,1)S(1)}, s32[]{:S(2)}) async-start(s8[22544384]{0:T(1024)(128)(4,1)} %bitcast.157), calls=%async_computation.11 | async-start | bytes 8388608
  2707.0 36.3 %slice-start.6 = ((s8[22544384]{0:T(1024)(128)(4,1)}), s8[4194304]{0:T(1024)(128)(4,1)S(1)}, s32[]{:S(2)}) async-start(s8[22544384]{0:T(1024)(128)(4,1)} %bitcast.157), calls=%async_computation.12 | async-start | bytes 8388608
  (46 other events, 849.2 us)
Sparse Core Ops, SparseCore 0:
  1172.7 64.9 all-reduce.4
  1240.9 1466.0 all-reduce.6
where the time goes:
time: 2770 us; the launch traced here: 2760 us
  waiting for transfers between devices  1670 us (60%)
  matrix products  657 us (24%)
  blocking collectives  317 us (11%)
  local copies, waits for them, and re-layouts  50.3 us (2%)
  other arithmetic  31.7 us (1%)
    psum x1, waiting for transfers between devices, local_step(): dw_gate = lax.psum(dw_gate, 'dp')  1010 us
    all_to_all x1, blocking collectives, local_step(): lax.all_to_all(grad_hid, 'ep', 0, 0, tiled=True)  283 us
    all_to_all x1, waiting for transfers between devices, local_step(): lax.all_to_all(grad_buf.reshape(n_ep, local_exp, slot_cap, d_model), 'ep'...  241 us
    all_to_all x1, waiting for transfers between devices, local_step(): lax.all_to_all(hid_buf.reshape(n_ep, local_exp, slot_cap, d_model), 'ep',...  230 us
    all_to_all x1, waiting for transfers between devices, local_step(): lax.all_to_all(exp_out, 'ep', 0, 0, tiled=True)  186 us
    dot_general x1, matrix products, local_step(): jnp.einsum('sgcd,gdf->sgcf', hid_recv, w_gate, preferred_element_type=f32)  64.7 us
  transfers between devices with their start and end apart: 5, of which 4 were waited for; matrix products, arithmetic and copies ran while one was open for 13% of the time, Pallas kernels for 0%

commit v1 on v0

v1 whole, which is shorter than its diff:
```python
import functools

import jax
import jax.numpy as jnp
from jax import lax
from jax.experimental import pallas as pl
from jax.experimental.pallas import tpu as pltpu
from jax.sharding import PartitionSpec as P

LN_EPS = 1e-5
N_CHUNK = 3
FF_BLOCK = 352
COL_BLOCK = 512
OUT_BLOCK = 256
SRC_BLOCK = 4
VMEM_BYTES = 60 * 1024 * 1024
f32 = jnp.float32
bf16 = jnp.bfloat16


def layer_norm(x_rows, ln_weight, ln_bias):
    x_float = x_rows.astype(jnp.float32)
    centered = x_float - jnp.mean(x_float, axis=-1, keepdims=True)
    inv_std = lax.rsqrt(jnp.mean(centered * centered, axis=-1, keepdims=True) + LN_EPS)
    x_hat = centered * inv_std
    hidden = (x_hat * ln_weight.astype(jnp.float32) + ln_bias.astype(jnp.float32)).astype(jnp.bfloat16)
    return hidden, x_hat, inv_std


def layer_norm_back(grad_h, x_hat, inv_std, ln_weight):
    scaled = grad_h * ln_weight.astype(jnp.float32)
    return inv_std * (scaled - jnp.mean(scaled, axis=-1, keepdims=True)
                      - x_hat * jnp.mean(scaled * x_hat, axis=-1, keepdims=True))


def masked_gate(logits, allowed, choice):
    expert_ids = jnp.arange(logits.shape[-1])
    prob_all = jax.nn.softmax(jnp.where(allowed, logits, -1e30), axis=-1)
    picked = (choice[:, None] == expert_ids[None, :]).astype(jnp.float32)
    return jnp.sum(prob_all * picked, axis=-1), prob_all, picked


def dot(lhs, rhs, lhs_dim, rhs_dim):
    return lax.dot_general(lhs, rhs, (((lhs_dim,), (rhs_dim,)), ((), ())), preferred_element_type=f32)


def once(shape, index):
    return pl.BlockSpec(shape, index, pipeline_mode=pl.Buffered(1))


def cost(flops, moved):
    return pl.CostEstimate(flops=flops, bytes_accessed=moved, transcendentals=0)


def mid_kernel(plane_ref, hid_ref, grad_ref, gate_ref, up_ref, down_ref, *refs):
    act_ref, back_gate_ref, back_up_ref = refs[-3:]
    rows = hid_ref.shape[-2]

    def block(i, carry):
        cols = pl.ds(pl.multiple_of(i * COL_BLOCK, COL_BLOCK), COL_BLOCK)
        hid = hid_ref[0, cols, :]
        pre_gate = dot(gate_ref[...], hid, 1, 1)
        pre_up = dot(up_ref[...], hid, 1, 1)
        grad_inner = dot(down_ref[...], grad_ref[0, cols, :], 1, 1)
        sig_gate = jax.nn.sigmoid(pre_gate)
        silu_gate = pre_gate * sig_gate
        act_ref[0, :, cols] = (silu_gate * pre_up).astype(bf16)
        back_gate_ref[0, :, cols] = (grad_inner * pre_up * sig_gate * (1.0 + pre_gate * (1.0 - sig_gate))).astype(bf16)
        back_up_ref[0, :, cols] = (grad_inner * silu_gate).astype(bf16)
        return carry

    lax.fori_loop(0, rows // COL_BLOCK, block, 0)


def expert_mid(source, target, hid, grad, weights, earlier=()):
    rows, d_model = hid.shape[1:]
    ff = weights[0].shape[0]
    planes = jnp.stack([source, target]).astype(jnp.int32)
    row_spec = once((1, rows, d_model), lambda j, p: (p[0], 0, 0))
    weight_spec = pl.BlockSpec((FF_BLOCK, d_model), lambda j, p: (j, 0))
    out_spec = pl.BlockSpec((1, FF_BLOCK, rows), lambda j, p: (p[1], j, 0))
    shape = jax.ShapeDtypeStruct((2, ff, rows), bf16)
    return pl.pallas_call(
        mid_kernel,
        grid_spec=pltpu.PrefetchScalarGridSpec(
            num_scalar_prefetch=1, grid=(pl.cdiv(ff, FF_BLOCK),),
            in_specs=[row_spec] * 2 + [weight_spec] * 3 + [pl.BlockSpec(memory_space=pl.ANY)] * len(earlier),
            out_specs=[out_spec] * 3),
        out_shape=[shape] * 3,
        input_output_aliases={6 + k: k for k in range(len(earlier))},
        cost_estimate=cost(6 * rows * ff * d_model, 4 * rows * d_model + 6 * ff * (d_model + rows)),
        compiler_params=pltpu.CompilerParams(vmem_limit_bytes=VMEM_BYTES),
        name="expert_mid")(planes, hid, grad, *weights, *earlier)


def back_kernel(count, plane_ref, *refs):
    lhs_refs, weight_refs, out_ref, turned = refs[:count], refs[count:2 * count], refs[-1 - count], refs[-count:]
    d_model = out_ref.shape[-1]
    for lhs_ref, turned_ref in zip(lhs_refs, turned):
        turned_ref[...] = lhs_ref[0].T

    def block(i, carry):
        cols = pl.ds(pl.multiple_of(i * COL_BLOCK, COL_BLOCK), COL_BLOCK)
        total = dot(turned[0][...], weight_refs[0][:, cols], 1, 0)
        for turned_ref, weight_ref in zip(turned[1:], weight_refs[1:]):
            total = total + dot(turned_ref[...], weight_ref[:, cols], 1, 0)
        out_ref[:, :, cols] = total.astype(bf16).reshape(out_ref.shape[:2] + (COL_BLOCK,))
        return carry

    lax.fori_loop(0, d_model // COL_BLOCK, block, 0)


def expert_back(plane, lhs, weights, chunk, n_src, slot_cap, earlier=()):
    ff, d_model = weights[0].shape
    rows = lhs[0].shape[2]
    part = rows // n_src
    count = len(lhs)
    block = SRC_BLOCK * part
    return pl.pallas_call(
        functools.partial(back_kernel, count),
        grid_spec=pltpu.PrefetchScalarGridSpec(
            num_scalar_prefetch=1, grid=(n_src // SRC_BLOCK,),
            in_specs=[pl.BlockSpec((1, ff, block), lambda j, p: (p[0], 0, j))] * count
            + [once((ff, d_model), lambda j, p: (0, 0))] * count + [pl.BlockSpec(memory_space=pl.ANY)] * len(earlier),
            out_specs=pl.BlockSpec((SRC_BLOCK, part, d_model), lambda j, p: (j, chunk, 0)),
            scratch_shapes=[pltpu.VMEM((block, ff), bf16)] * count),
        out_shape=jax.ShapeDtypeStruct((n_src, slot_cap, d_model), bf16),
        input_output_aliases={1 + 2 * count + k: k for k in range(len(earlier))},
        cost_estimate=cost(2 * count * rows * ff * d_model, 2 * (count * ff * (d_model + rows) + rows * d_model)),
        compiler_params=pltpu.CompilerParams(vmem_limit_bytes=VMEM_BYTES),
        name="expert_back")(plane.reshape(1).astype(jnp.int32), *lhs, *weights, *earlier)


def grads_kernel(act_ref, back_gate_ref, back_up_ref, hid_ref, grad_ref, *refs):
    ff = act_ref.shape[1]
    half = ff // 2

    def block(i, carry):
        rows = pl.ds(pl.multiple_of(i * half, 16), half)
        for k, (lhs_ref, rhs_ref) in enumerate(((back_gate_ref, hid_ref), (back_up_ref, hid_ref), (act_ref, grad_ref))):
            total = dot(lhs_ref[0, rows, :], rhs_ref[0], 1, 0) + dot(lhs_ref[1, rows, :], rhs_ref[1], 1, 0)
            if len(refs) > 3:
                total = total + refs[k][rows, :]
            refs[-3 + k][rows, :] = total
        return carry

    lax.fori_loop(0, 2, block, 0)


def expert_grads(act, back_gate, back_up, hid_all, grad_all, earlier=()):
    planes, rows, d_model = hid_all.shape
    ff = act.shape[1]
    lhs_spec = once((planes, ff, rows), lambda j: (0, 0, 0))
    rhs_spec = pl.BlockSpec((planes, rows, OUT_BLOCK), lambda j: (0, 0, j))
    out_spec = pl.BlockSpec((ff, OUT_BLOCK), lambda j: (0, j))
    return pl.pallas_call(
        grads_kernel,
        grid=(d_model // OUT_BLOCK,),
        in_specs=[lhs_spec] * 3 + [rhs_spec] * 2 + [out_spec] * len(earlier),
        out_specs=[out_spec] * 3,
        out_shape=[jax.ShapeDtypeStruct((ff, d_model), f32)] * 3,
        input_output_aliases={5 + k: k for k in range(len(earlier))},
        cost_estimate=cost(12 * rows * ff * d_model, 12 * ff * (rows + 2 * d_model) + 8 * rows * d_model),
        compiler_params=pltpu.CompilerParams(vmem_limit_bytes=VMEM_BYTES),
        name="expert_grads")(act, back_gate, back_up, hid_all, grad_all, *earlier)


def solution(mesh):
    n_ep = mesh.shape['ep']
    tok_spec = P(('dp', 'ep'), None)
    row_spec = P(('dp', 'ep'))
    exp_spec = P('ep', None, None)

    def local_step(tok_x, tok_dy, exp_first, exp_second, eligible, slot_first, slot_second,
                   ln_weight, ln_bias, router, w_gate, w_up, w_down):
        n_local, d_model = tok_x.shape
        n_exp = eligible.shape[1]
        weights = (w_gate[0].T, w_up[0].T, w_down[0])
        slot_cap = 3 * n_local // n_exp
        part = slot_cap // N_CHUNK
        dp_index = lax.axis_index('dp')
        hidden, x_hat, inv_std = layer_norm(tok_x, ln_weight, ln_bias)
        logits = jnp.dot(hidden, router, preferred_element_type=f32)
        expert_ids = jnp.arange(n_exp)
        allowed = eligible > 0
        gate_one, prob_one, pick_one = masked_gate(logits, allowed, exp_first)
        gate_two, prob_two, pick_two = masked_gate(logits, allowed & (expert_ids[None, :] != exp_first[:, None]), exp_second)

        def select(choice, slot, start, part):
            rel = slot - start
            pos = jnp.where((rel >= 0) & (rel < part), choice * part + rel, -1)
            return pos[:, None] == jnp.arange(n_exp * part)[None, :]

        def exchange(buf, part):
            return lax.all_to_all(buf.reshape(n_ep, part, d_model), 'ep', 0, 0, tiled=True)

        last = []

        def chain(*arrays):
            tied = lax.optimization_barrier(tuple(arrays) + tuple(last))
            return tied[:len(arrays)]

        def done(*arrays):
            last[:] = arrays

        dy_float = tok_dy.astype(f32)
        hid_buf, grad_buf = [], []
        for c in range(N_CHUNK):
            one, two = select(exp_first, slot_first, c * part, part), select(exp_second, slot_second, c * part, part)
            sel_both = one.astype(bf16) + two.astype(bf16)
            gate_row = jnp.sum(jnp.where(one, gate_one[:, None], 0.0) + jnp.where(two, gate_two[:, None], 0.0), axis=0)
            hid_in, = chain(hidden)
            hid_buf.append(dot(sel_both, hid_in, 0, 0).astype(bf16))
            done(hid_buf[-1])
            dy_in, = chain(tok_dy)
            grad_buf.append((dot(sel_both, dy_in, 0, 0) * gate_row[:, None]).astype(bf16))
            done(grad_buf[-1])
        hid_recv, grad_recv, hid_all, grad_all = [], [], [], []
        previous = []
        for c in range(N_CHUNK):
            for buf, recv, both in ((hid_buf[c], hid_recv, hid_all), (grad_buf[c], grad_recv, grad_all)):
                buf = lax.optimization_barrier((buf, *previous))[0]
                recv.append(exchange(buf, part).reshape(n_exp * part, d_model))
                previous = [recv[-1]]
                both.append(lax.all_gather(recv[-1], 'dp'))

        middle = [None] * N_CHUNK
        exp_out, grad_hid, weight_grads = (), (), ()

        def mid_own(c):
            rows, grads = chain(hid_recv[c][None], grad_recv[c][None])
            middle[c] = expert_mid(0 * dp_index, dp_index, rows, grads, weights)
            done(*middle[c])

        def mid_far(c):
            rows, grads = chain(hid_all[c], grad_all[c])
            middle[c] = expert_mid(1 - dp_index, 1 - dp_index, rows, grads, weights, middle[c])
            done(*middle[c])

        def rows_back(lhs, lhs_weights, c, earlier):
            lhs = chain(*lhs)
            out = expert_back(dp_index, lhs, lhs_weights, c, n_ep, slot_cap, earlier)
            done(out)
            return (out,)

        def weight_back(c, earlier):
            act, back_gate, back_up = chain(*middle[c])
            out = expert_grads(act, back_gate, back_up, hid_all[c], grad_all[c], earlier)
            done(*out)
            return out

        for c in range(N_CHUNK):
            if c == N_CHUNK - 1:
                mid_far(0)
            mid_own(c)
            exp_out = rows_back(middle[c][:1], weights[2:], c, exp_out)
            grad_hid = rows_back(middle[c][1:], weights[:2], c, grad_hid)
        out_back = exchange(lax.optimization_barrier((exp_out[0], *previous))[0], slot_cap).reshape(-1, d_model)
        hid_back = exchange(lax.optimization_barrier((grad_hid[0], out_back))[0], slot_cap).reshape(-1, d_model)
        weight_grads = weight_back(0, weight_grads)
        mid_far(1)
        weight_grads = weight_back(1, weight_grads)
        out_in, = chain(out_back)
        sel_one = select(exp_first, slot_first, 0, slot_cap).astype(bf16)
        sel_two = select(exp_second, slot_second, 0, slot_cap).astype(bf16)
        out_one = dot(sel_one, out_in, 1, 0)
        out_two = dot(sel_two, out_in, 1, 0)
        y_mix = gate_one[:, None] * out_one + gate_two[:, None] * out_two
        out_tok = (tok_x.astype(f32) + y_mix).astype(bf16)
        dgate_one = jnp.sum(dy_float * out_one, axis=-1)
        dgate_two = jnp.sum(dy_float * out_two, axis=-1)
        d_logits = ((dgate_one * gate_one)[:, None] * (pick_one - prob_one)
                    + (dgate_two * gate_two)[:, None] * (pick_two - prob_two)).astype(bf16)
        d_router = jnp.einsum('td,te->de', hidden, d_logits, preferred_element_type=f32)
        done(out_tok, d_router)
        hid_in, = chain(hid_back)
        grad_exp = dot(sel_one + sel_two, hid_in, 1, 0)
        grad_h = jnp.einsum('te,de->td', d_logits, router, preferred_element_type=f32) + grad_exp
        d_ln_weight = jnp.sum(grad_h * x_hat, axis=0)
        d_ln_bias = jnp.sum(grad_h, axis=0)
        dx_tok = (dy_float + layer_norm_back(grad_h, x_hat, inv_std, ln_weight)).astype(bf16)
        done(dx_tok)
        mid_far(2)
        dw_gate, dw_up, dw_down = weight_back(2, weight_grads)
        d_router = lax.psum(d_router, ('dp', 'ep'))
        d_ln_weight = lax.psum(d_ln_weight, ('dp', 'ep'))
        d_ln_bias = lax.psum(d_ln_bias, ('dp', 'ep'))
        return out_tok, dx_tok, dw_gate.T[None], dw_up.T[None], dw_down[None], d_router, d_ln_weight, d_ln_bias

    return jax.shard_map(
        local_step, mesh=mesh,
        in_specs=(tok_spec, tok_spec, row_spec, row_spec, tok_spec, row_spec, row_spec,
                  P(), P(), P(), exp_spec, exp_spec, exp_spec),
        out_specs=(tok_spec, tok_spec, exp_spec, exp_spec, exp_spec, P(), P(), P()),
        check_vma=False)
```

time: 2770 us -> 1670 us (0.60)
  waiting for transfers between devices: 1670 us -> 214 us
  Pallas kernels: 0 us -> 744 us
  matrix products: 657 us -> 204 us
  blocking collectives: 317 us -> 428 us
  local copies, waits for them, and re-layouts: 50.3 us -> 3.25 us
    psum x1 -> x0, waiting for transfers between devices: 1010 us -> none  [local_step(): dw_gate = lax.psum(dw_gate, 'dp')]
    pallas_call x0 -> x15, Pallas kernels: none -> 744 us  [the longest x6 295 us: expert_mid(): pl.pallas_call(mid_kernel, grid_spec=pltpu.PrefetchScalarGridSpec(num_sca...]
    dot_general x15 -> x9, matrix products: 635 us -> 180 us  [dot(): lax.dot_general(lhs, rhs, (((lhs_dim,), (rhs_dim,)), ((), ())), preferred...]
    all_to_all x3 -> x4, waiting for transfers between devices: 657 us -> 213 us  [exchange(): lax.all_to_all(buf.reshape(n_ep, part, d_model), 'ep', 0, 0, tiled=True)]
    all_to_all x1 -> x4, blocking collectives: 283 us -> 396 us  [exchange(): lax.all_to_all(buf.reshape(n_ep, part, d_model), 'ep', 0, 0, tiled=True)]
    unnamed x134 -> x77, local copies, waits for them, and re-layouts: 50.3 us -> 3.25 us
  transfers between devices with their start and end apart: 5 -> 11, of which waited for: 4 -> 2; matrix products, arithmetic and copies ran while one was open for 13% -> 12% of each run, Pallas kernels for 0% -> 45%
where the time goes in v1:
time: 1670 us
  Pallas kernels  744 us (45%)
  blocking collectives  428 us (26%)
  waiting for transfers between devices  214 us (13%)
  matrix products  204 us (12%)
  other arithmetic  33.8 us (2%)
  starting transfers between devices  23.3 us (1%)
    all_to_all x4, blocking collectives, exchange(): lax.all_to_all(buf.reshape(n_ep, part, d_model), 'ep', 0, 0, tiled=True)  396 us
    pallas_call x6, Pallas kernels, expert_mid(): pl.pallas_call(mid_kernel, grid_spec=pltpu.PrefetchScalarGridSpec(num_sca...  295 us
    pallas_call x3, Pallas kernels, expert_grads(): pl.pallas_call(grads_kernel, grid=(d_model // OUT_BLOCK,), in_specs=[lhs_...  258 us
    all_to_all x4, waiting for transfers between devices, exchange(): lax.all_to_all(buf.reshape(n_ep, part, d_model), 'ep', 0, 0, tiled=True)  213 us
    pallas_call x6, Pallas kernels, expert_back(): pl.pallas_call(functools.partial(back_kernel, count), grid_spec=pltpu.Pre...  192 us
    dot_general x9, matrix products, dot(): lax.dot_general(lhs, rhs, (((lhs_dim,), (rhs_dim,)), ((), ())), preferred...  180 us
  transfers between devices with their start and end apart: 11, of which 2 were waited for; matrix products, arithmetic and copies ran while one was open for 12% of the time, Pallas kernels for 45%

profile of v1, /device:TPU:0, one launch (start us, length us, event | category | flops | bytes accessed | tf_op | source)
XLA Modules:
  0.0 1666.1 jit_solution(14978895107697145852)
XLA Ops:
  50.2 99.2 %all_to_all.40 = bf16[8,128,4096]{2,1,0:T(8,128)(2,1)} all-to-all(bf16[8,128,4096]{2,1,0:T(8,128)(2,1)S(1)} %bitcast.64), channel_id=1, replica_groups=mesh['dp'=2,'ep'=8] {'ep'}, dimensions={0} | all-to-all | bytes 16777216 | tf_op jit(solution)/shard_map/all_to_all | solution.py:195
  149.5 99.4 %all_to_all.41 = bf16[8,128,4096]{2,1,0:T(8,128)(2,1)} all-to-all(bf16[8,128,4096]{2,1,0:T(8,128)(2,1)} %bitcast.62), channel_id=1, replica_groups=mesh['dp'=2,'ep'=8] {'ep'}, dimensions={0} | all-to-all | bytes 16777216 | tf_op jit(solution)/shard_map/all_to_all | solution.py:195
  276.9 97.3 %all_to_all.42 = bf16[8,128,4096]{2,1,0:T(8,128)(2,1)} all-to-all(bf16[8,128,4096]{2,1,0:T(8,128)(2,1)S(1)} %bitcast.65), channel_id=1, replica_groups=mesh['dp'=2,'ep'=8] {'ep'}, dimensions={0} | all-to-all | bytes 16777216 | tf_op jit(solution)/shard_map/all_to_all | solution.py:195
  374.2 99.6 %all_to_all.43 = bf16[8,128,4096]{2,1,0:T(8,128)(2,1)} all-to-all(bf16[8,128,4096]{2,1,0:T(8,128)(2,1)} %bitcast.63), channel_id=1, replica_groups=mesh['dp'=2,'ep'=8] {'ep'}, dimensions={0} | all-to-all | bytes 16777216 | tf_op jit(solution)/shard_map/all_to_all | solution.py:195
  510.3 48.9 %expert_mid.6 = (bf16[2,1376,1024]{2,1,0:T(8,128)(2,1)}, bf16[2,1376,1024]{2,1,0:T(8,128)(2,1)}, bf16[2,1376,1024]{2,1,0:T(8,128)(2,1)}) custom-call(s32[2]{0:T(128)} %pad_add_fusion.plane_ref, bf16[1,1024,4096]{2,1,0:T(8,128)(2,1)} %bitcast.59, bf16[1,1024,4096]{2,1,0:T(8,128)(2,1)} %bitcast.57, bf16[1376,4096]{1,0:T(8,128)(2,1)} %bitcast.68, ...), custom_call_target="tpu_custom_call" | custom-call | flops 34628173824 | bytes 59047936 | tf_op jit(solution)/shard_map/expert_mid/pallas_call | solution.py:83
  559.3 23.3 %expert_back.6.refs_2_ = bf16[8,384,4096]{2,1,0:T(8,128)(2,1)} custom-call(s32[1]{0:T(128)} %bitcast.plane_ref, bf16[2,1376,1024]{2,1,0:T(8,128)(2,1)} %get-tuple-element.77.refs_0_, bf16[1376,4096]{1,0:T(8,128)(2,1)} %bitcast.44), custom_call_target="tpu_custom_call" | custom-call | flops 11542724608 | bytes 22478848 | tf_op jit(solution)/shard_map/expert_back/pallas_call | solution.py:119
  582.5 40.7 %expert_back.7.refs_4_ = bf16[8,384,4096]{2,1,0:T(8,128)(2,1)} custom-call(s32[1]{0:T(128)} %bitcast.plane_ref, bf16[2,1376,1024]{2,1,0:T(8,128)(2,1)} %get-tuple-element.78.refs_0_.refs_1_, bf16[2,1376,1024]{2,1,0:T(8,128)(2,1)} %get-tuple-element.79.refs_1_.refs_2_, bf16[1376,4096]{1,0:T(8,128)(2,1)} %bitcast.69, bf16[1376,4096]{1,0:T(8,128)(2,1)} %bitcast.78), custom_call_target="tpu_custom_call" | custom-call | flops 23085449216 | bytes 36569088 | tf_op jit(solution)/shard_map/expert_back/pallas_call | solution.py:119
  628.2 49.2 %expert_mid.7 = (bf16[2,1376,1024]{2,1,0:T(8,128)(2,1)}, bf16[2,1376,1024]{2,1,0:T(8,128)(2,1)}, bf16[2,1376,1024]{2,1,0:T(8,128)(2,1)}) custom-call(s32[2]{0:T(128)} %pad_add_fusion.plane_ref, bf16[1,1024,4096]{2,1,0:T(8,128)(2,1)} %bitcast.55, bf16[1,1024,4096]{2,1,0:T(8,128)(2,1)} %bitcast.53, bf16[1376,4096]{1,0:T(8,128)(2,1)} %bitcast.70, ...), custom_call_target="tpu_custom_call" | custom-call | flops 34628173824 | bytes 59047936 | tf_op jit(solution)/shard_map/expert_mid/pallas_call | solution.py:83
  700.6 40.8 %expert_back.9.refs_4_ = bf16[8,384,4096]{2,1,0:T(8,128)(2,1)} custom-call(s32[1]{0:T(128)} %bitcast.plane_ref, bf16[2,1376,1024]{2,1,0:T(8,128)(2,1)} %get-tuple-element.86.refs_0_.refs_1_, bf16[2,1376,1024]{2,1,0:T(8,128)(2,1)} %get-tuple-element.87.refs_1_.refs_2_, bf16[1376,4096]{1,0:T(8,128)(2,1)} %bitcast.71, ...), custom_call_target="tpu_custom_call", output_to_operand_aliasing={{}: (5, {})} | custom-call | flops 23085449216 | bytes 36569088 | tf_op jit(solution)/shard_map/expert_back/pallas_call | solution.py:119
  741.4 48.9 %expert_mid.8 = (bf16[2,1376,1024]{2,1,0:T(8,128)(2,1)}, bf16[2,1376,1024]{2,1,0:T(8,128)(2,1)}, bf16[2,1376,1024]{2,1,0:T(8,128)(2,1)}) custom-call(s32[2]{0:T(128)} %pad_add_fusion.1.plane_ref, bf16[2,1024,4096]{2,1,0:T(8,128)(2,1)} %all-gather.7.cloned.1.call-done.hid_ref, ...), custom_call_target="tpu_custom_call", output_to_operand_aliasing={{0}: (6, {}), {1}: (7, {}), {2}: (8, {})} | custom-call | flops 34628173824 | bytes 59047936 | tf_op jit(solution)/shard_map/expert_mid/pallas_call | solution.py:83
  790.3 49.5 %expert_mid.9 = (bf16[2,1376,1024]{2,1,0:T(8,128)(2,1)}, bf16[2,1376,1024]{2,1,0:T(8,128)(2,1)}, bf16[2,1376,1024]{2,1,0:T(8,128)(2,1)}) custom-call(s32[2]{0:T(128)} %pad_add_fusion.plane_ref, bf16[1,1024,4096]{2,1,0:T(8,128)(2,1)} %bitcast.2.hid_ref, bf16[1,1024,4096]{2,1,0:T(8,128)(2,1)} %bitcast.4.grad_ref, bf16[1376,4096]{1,0:T(8,128)(2,1)} %bitcast.73, ...), custom_call_target="tpu_custom_call" | custom-call | flops 34628173824 | bytes 59047936 | tf_op jit(solution)/shard_map/expert_mid/pallas_call | solution.py:83
  839.8 23.3 %expert_back.10 = bf16[8,384,4096]{2,1,0:T(8,128)(2,1)} custom-call(s32[1]{0:T(128)} %bitcast.plane_ref, bf16[2,1376,1024]{2,1,0:T(8,128)(2,1)} %get-tuple-element.98.refs_0_, bf16[1376,4096]{1,0:T(8,128)(2,1)} %bitcast.49, bf16[8,384,4096]{2,1,0:T(8,128)(2,1)} %expert_back.8.refs_2_), custom_call_target="tpu_custom_call", output_to_operand_aliasing={{}: (3, {})} | custom-call | flops 11542724608 | bytes 22478848 | tf_op jit(solution)/shard_map/expert_back/pallas_call | solution.py:119
  870.0 40.8 %expert_back.11 = bf16[8,384,4096]{2,1,0:T(8,128)(2,1)} custom-call(s32[1]{0:T(128)} %bitcast.plane_ref, bf16[2,1376,1024]{2,1,0:T(8,128)(2,1)} %get-tuple-element.99.refs_0_.refs_1_, bf16[2,1376,1024]{2,1,0:T(8,128)(2,1)} %get-tuple-element.100.refs_1_.refs_2_, bf16[1376,4096]{1,0:T(8,128)(2,1)} %bitcast.74, ...), custom_call_target="tpu_custom_call", output_to_operand_aliasing={{}: (5, {})} | custom-call | flops 23085449216 | bytes 36569088 | tf_op jit(solution)/shard_map/expert_back/pallas_call | solution.py:119
  910.8 84.3 %expert_grads.3 = (f32[1376,4096]{1,0:T(8,128)}, f32[1376,4096]{1,0:T(8,128)}, f32[1376,4096]{1,0:T(8,128)}) custom-call(bf16[2,1376,1024]{2,1,0:T(8,128)(2,1)} %get-tuple-element.101.act_ref, bf16[2,1376,1024]{2,1,0:T(8,128)(2,1)} %get-tuple-element.102.back_gate_ref, bf16[2,1376,1024]{2,1,0:T(8,128)(2,1)} %get-tuple-element.103.back_up_ref, ...), custom_call_target="tpu_custom_call" | custom-call | flops 69256347648 | bytes 185729024 | tf_op jit(solution)/shard_map/expert_grads/pallas_call | solution.py:156
  995.1 148.3 %all-to-all-done.6 = bf16[8,384,4096]{2,1,0:T(8,128)(2,1)} async-done(((bf16[8,384,4096]{2,1,0:T(8,128)(2,1)}), bf16[8,384,4096]{2,1,0:T(8,128)(2,1)}, u32[]{:S(2)}, u32[]{:S(2)}) %all-to-all-start.6) | async-done | bytes 25165856 | tf_op jit(solution)/shard_map/all_to_all | solution.py:195
  1149.9 49.1 %expert_mid.10 = (bf16[2,1376,1024]{2,1,0:T(8,128)(2,1)}, bf16[2,1376,1024]{2,1,0:T(8,128)(2,1)}, bf16[2,1376,1024]{2,1,0:T(8,128)(2,1)}) custom-call(s32[2]{0:T(128)} %pad_add_fusion.1.plane_ref, bf16[2,1024,4096]{2,1,0:T(8,128)(2,1)} %all-gather.11.cloned.1.call-done.hid_ref, ...), custom_call_target="tpu_custom_call", output_to_operand_aliasing={{0}: (6, {}), {1}: (7, {}), {2}: (8, {})} | custom-call | flops 34628173824 | bytes 59047936 | tf_op jit(solution)/shard_map/expert_mid/pallas_call | solution.py:83
  1199.1 86.7 %expert_grads.4 = (f32[1376,4096]{1,0:T(8,128)}, f32[1376,4096]{1,0:T(8,128)}, f32[1376,4096]{1,0:T(8,128)}) custom-call(bf16[2,1376,1024]{2,1,0:T(8,128)(2,1)} %get-tuple-element.109.act_ref, bf16[2,1376,1024]{2,1,0:T(8,128)(2,1)} %get-tuple-element.110.back_gate_ref, ...), custom_call_target="tpu_custom_call", output_to_operand_aliasing={{0}: (5, {}), {1}: (6, {}), {2}: (7, {})} | custom-call | flops 69256347648 | bytes 185729024 | tf_op jit(solution)/shard_map/expert_grads/pallas_call | solution.py:156
  1285.8 31.5 %fusion.18 = f32[1024,4096]{1,0:T(8,128)} fusion(bf16[3072,4096]{1,0:T(8,128)(2,1)} %bitcast.19, s32[1024]{0:T(1024)S(1)} %copy-done.34), kind=kOutput, calls=%fused_computation.29 | convolution fusion | flops 25772949504 | bytes 41947136 | tf_op jit(solution)/shard_map/dot_general | solution.py:44
  1317.4 36.5 %fusion.14 = (f32[1024]{0:T(1024)S(1)}, f32[1024]{0:T(1024)S(1)}, bf16[1024,4096]{1,0:T(8,128)(2,1)}) fusion(bf16[1024,4096]{1,0:T(8,128)(2,1)} %param.14, f32[1024,4096]{1,0:T(8,128)} %fusion.18, f32[1024]{0:T(1024)S(1)} %copy-done.29, f32[1024]{0:T(1024)S(1)} %copy-done.27, bf16[1024,4096]{1,0:T(8,128)(2,1)} %param.13, bf16[3072,4096]{1,0:T(8,128)(2,1)} %bitcast.19, ...), kind=kOutput, calls=%fused_computation.20 | convolution fusion | flops 25819086848 | bytes 67129344 | tf_op jit(solution)/shard_map/dot_general | solution.py:44
  1359.2 64.6 %all-to-all-done.7 = bf16[8,384,4096]{2,1,0:T(8,128)(2,1)} async-done(((bf16[8,384,4096]{2,1,0:T(8,128)(2,1)}), bf16[8,384,4096]{2,1,0:T(8,128)(2,1)}, u32[]{:S(2)}, u32[]{:S(2)}) %all-to-all-start.7) | async-done | bytes 25165856 | tf_op jit(solution)/shard_map/all_to_all | solution.py:195
  1423.8 31.8 %fusion.22 = f32[1024,4096]{1,0:T(8,128)} fusion(bf16[3072,4096]{1,0:T(8,128)(2,1)} %bitcast.22, s32[1024]{0:T(1024)S(1)} %copy-done.34, s32[1024]{0:T(1024)S(1)} %copy-done.35), kind=kOutput, calls=%fused_computation.38 | convolution fusion | flops 25794969600 | bytes 41951232 | tf_op jit(solution)/shard_map/dot_general | solution.py:44
  1488.5 49.2 %expert_mid.11 = (bf16[2,1376,1024]{2,1,0:T(8,128)(2,1)}, bf16[2,1376,1024]{2,1,0:T(8,128)(2,1)}, bf16[2,1376,1024]{2,1,0:T(8,128)(2,1)}) custom-call(s32[2]{0:T(128)} %pad_add_fusion.1.plane_ref, bf16[2,1024,4096]{2,1,0:T(8,128)(2,1)} %all-gather.15.cloned.1.call-done.hid_ref, ...), custom_call_target="tpu_custom_call", output_to_operand_aliasing={{0}: (6, {}), {1}: (7, {}), {2}: (8, {})} | custom-call | flops 34628173824 | bytes 59047936 | tf_op jit(solution)/shard_map/expert_mid/pallas_call | solution.py:83
  1537.7 86.7 %expert_grads.5 = (f32[1376,4096]{1,0:T(8,128)}, f32[1376,4096]{1,0:T(8,128)}, f32[1376,4096]{1,0:T(8,128)}) custom-call(bf16[2,1376,1024]{2,1,0:T(8,128)(2,1)} %get-tuple-element.120.act_ref, bf16[2,1376,1024]{2,1,0:T(8,128)(2,1)} %get-tuple-element.121.back_gate_ref, ...), custom_call_target="tpu_custom_call", output_to_operand_aliasing={{0}: (5, {}), {1}: (6, {}), {2}: (7, {})} | custom-call | flops 69256347648 | bytes 185729024 | tf_op jit(solution)/shard_map/expert_grads/pallas_call | solution.py:156
  1624.4 32.8 %all-reduce = (f32[4096]{0:T(1024)}, f32[4096]{0:T(1024)}) all-reduce(f32[4096]{0:T(1024)S(1)} %get-tuple-element.126, f32[4096]{0:T(1024)S(1)} %get-tuple-element.129), channel_id=1, replica_groups=mesh['dp'=2,'ep'=8] {'dp','ep'}, use_global_device_ids=true, to_apply=%region_17.18 | all-reduce | flops 8192 | bytes 65536 | tf_op jit(solution)/shard_map/psum | solution.py:286
  (134 shorter events, 188.6 us)
Async XLA Ops:
  7.2 734.2 %all-gather.9.cloned.1.call-start = ((), (), s32[]{:S(2)}) async-start(), calls=%async_computation.9 | async-start | bytes 25165824 | tf_op jit(solution)/shard_map/all_gather | solution.py:225
  149.5 591.9 %all-gather.7.cloned.1.call-start = ((), (), s32[]{:S(2)}) async-start(), calls=%async_computation.8 | async-start | bytes 25165824 | tf_op jit(solution)/shard_map/all_gather | solution.py:225
  248.9 746.1 %all-gather.13.cloned.1.call-start = ((), (), s32[]{:S(2)}) async-start(), calls=%async_computation.11 | async-start | bytes 25165824 | tf_op jit(solution)/shard_map/all_gather | solution.py:225
  374.2 620.9 %all-gather.11.cloned.1.call-start = ((), (), s32[]{:S(2)}) async-start(), calls=%async_computation.10 | async-start | bytes 25165824 | tf_op jit(solution)/shard_map/all_gather | solution.py:225
  504.0 119.2 %all-to-all-start.1 = ((bf16[8,128,4096]{2,1,0:T(8,128)(2,1)}), bf16[8,128,4096]{2,1,0:T(8,128)(2,1)}, u32[]{:S(2)}, u32[]{:S(2)}) async-start(bf16[8,128,4096]{2,1,0:T(8,128)(2,1)} %bitcast.61), calls=%async_computation.1 | async-start | bytes 16777216 | tf_op jit(solution)/shard_map/all_to_all | solution.py:195
  623.2 167.2 %all-to-all-start = ((bf16[8,128,4096]{2,1,0:T(8,128)(2,1)}), bf16[8,128,4096]{2,1,0:T(8,128)(2,1)}, u32[]{:S(2)}, u32[]{:S(2)}) async-start(bf16[8,128,4096]{2,1,0:T(8,128)(2,1)} %bitcast.60), calls=%async_computation | async-start | bytes 16777216 | tf_op jit(solution)/shard_map/all_to_all | solution.py:195
  628.2 860.3 %all-gather.17.cloned.1.call-start = ((), (), s32[]{:S(2)}) async-start(), calls=%async_computation.13 | async-start | bytes 25165824 | tf_op jit(solution)/shard_map/all_gather | solution.py:225
  863.0 280.4 %all-to-all-start.6 = ((bf16[8,384,4096]{2,1,0:T(8,128)(2,1)}), bf16[8,384,4096]{2,1,0:T(8,128)(2,1)}, u32[]{:S(2)}, u32[]{:S(2)}) async-start(bf16[8,384,4096]{2,1,0:T(8,128)(2,1)} %expert_back.10), calls=%async_computation.6 | async-start | bytes 50331648 | tf_op jit(solution)/shard_map/all_to_all | solution.py:195
  869.5 619.0 %all-gather.15.cloned.1.call-start = ((), (), s32[]{:S(2)}) async-start(), calls=%async_computation.12 | async-start | bytes 25165824 | tf_op jit(solution)/shard_map/all_gather | solution.py:225
  1143.4 280.4 %all-to-all-start.7 = ((bf16[8,384,4096]{2,1,0:T(8,128)(2,1)}), bf16[8,384,4096]{2,1,0:T(8,128)(2,1)}, u32[]{:S(2)}, u32[]{:S(2)}) async-start(bf16[8,384,4096]{2,1,0:T(8,128)(2,1)} %expert_back.11), calls=%async_computation.7 | async-start | bytes 50331648 | tf_op jit(solution)/shard_map/all_to_all | solution.py:195
  1149.9 507.3 %all-reduce.3.cloned.1.call-start = ((), (), s32[]{:S(2)}) async-start(), calls=%async_computation.14 | async-start | bytes 262144 | tf_op jit(solution)/shard_map/psum | solution.py:285
  1199.1 86.7 %copy-start.34 = (s32[1024]{0:T(1024)S(1)}, s32[1024]{0:T(1024)}, u32[]{:S(2)}) copy-start(s32[1024]{0:T(1024)} %get-tuple-element.148) | copy-start | bytes 12292
  1285.8 31.6 %copy-start.27 = (f32[1024]{0:T(1024)S(1)}, f32[1024]{0:T(1024)}, u32[]{:S(2)}) copy-start(f32[1024]{0:T(1024)} %copy-done.26) | copy-start | bytes 12292
  1317.3 36.6 %copy-start.4 = (f32[1024,8]{0,1:T(8,128)S(1)}, f32[1024,8]{0,1:T(8,128)}, u32[]{:S(2)}) copy-start(f32[1024,8]{0,1:T(8,128)} %copy-done.3) | copy-start | bytes 98308
  1317.3 36.6 %copy-start.6 = (pred[1024,8]{0,1:T(8,128)(4,1)S(1)}, pred[1024,8]{0,1:T(8,128)(4,1)}, u32[]{:S(2)}) copy-start(pred[1024,8]{0,1:T(8,128)(4,1)} %copy-done.5) | copy-start | bytes 24580
  1317.4 36.6 %copy-start.10 = (s32[1024]{0:T(1024)S(1)}, s32[1024]{0:T(1024)}, u32[]{:S(2)}) copy-start(s32[1024]{0:T(1024)} %param.15) | copy-start | bytes 12292
  1317.4 36.6 %copy-start.12 = (f32[1024]{0:T(1024)S(1)}, f32[1024]{0:T(1024)}, u32[]{:S(2)}) copy-start(f32[1024]{0:T(1024)} %copy-done.11) | copy-start | bytes 12292
  1317.4 36.6 %copy-start.14 = (f32[1024]{0:T(1024)S(1)}, f32[1024]{0:T(1024)}, u32[]{:S(2)}) copy-start(f32[1024]{0:T(1024)} %copy-done.13) | copy-start | bytes 12292
  1317.4 36.6 %copy-start.19 = (f32[1024]{0:T(1024)S(1)}, f32[1024]{0:T(1024)}, u32[]{:S(2)}) copy-start(f32[1024]{0:T(1024)} %copy-done.18) | copy-start | bytes 12292
  1317.4 36.6 %copy-start.21 = (s32[1024]{0:T(1024)S(1)}, s32[1024]{0:T(1024)}, u32[]{:S(2)}) copy-start(s32[1024]{0:T(1024)} %param.16) | copy-start | bytes 12292
  1317.4 36.6 %copy-start.23 = (f32[1024]{0:T(1024)S(1)}, f32[1024]{0:T(1024)}, u32[]{:S(2)}) copy-start(f32[1024]{0:T(1024)} %copy-done.22) | copy-start | bytes 12292
  1423.8 31.8 %copy-start.8 = (f32[4096]{0:T(1024)S(1)}, f32[4096]{0:T(1024)}, u32[]{:S(2)}) copy-start(f32[4096]{0:T(1024)} %copy-done.7) | copy-start | bytes 49156
  1423.8 31.8 %copy-start.16 = (f32[1024]{0:T(1024)S(1)}, f32[1024]{0:T(1024)}, u32[]{:S(2)}) copy-start(f32[1024]{0:T(1024)} %copy-done.15) | copy-start | bytes 12292
  1423.8 31.8 %copy-start.25 = (f32[1024]{0:T(1024)S(1)}, f32[1024]{0:T(1024)}, u32[]{:S(2)}) copy-start(f32[1024]{0:T(1024)} %copy-done.24) | copy-start | bytes 12292
  (25 other events, 214.4 us)
Sparse Core Ops, SparseCore 0:
  149.6 196.7 all-gather.8
  347.9 197.5 all-gather.6
  547.1 197.5 all-gather.12
  746.1 197.5 all-gather.10
  945.1 197.5 all-gather.16
  1144.1 197.5 all-gather.14
  1472.1 64.2 all-reduce.2
